TPU v7x, 32 devices: a whole 2x2x4 slice. The times are simulated.
32 devices in a mesh: stage: 8 (over z, y), expert: 4 (over x, core).
Axes of the slice: x: 2, y: 2, z: 4, core: 2. Of those that a mesh axis runs over, the one named last changes fastest.
Arguments:
- x_acts: bfloat16 [2, 8, 4096, 512], P(None, 'stage', 'expert')
- expert_ids: int32 [2, 8, 4096, 2], P(None, 'stage', 'expert')
- gate_wts: float32 [2, 8, 4096, 2], P(None, 'stage', 'expert')
- w_in: bfloat16 [8, 8, 512, 1792], P('stage', 'expert')
- w_up: bfloat16 [8, 8, 512, 1792], P('stage', 'expert')
- w_out: bfloat16 [8, 8, 1792, 512], P('stage', 'expert')
- d_out: bfloat16 [8, 4096, 512], P('stage', 'expert')
Outputs:
- output 1: bfloat16 [8, 4096, 512], P('stage', 'expert')
- output 2: bfloat16 [8, 4096, 512], P('stage', 'expert')
- output 3: bfloat16 [8, 8, 512, 1792], P('stage', 'expert')
- output 4: bfloat16 [8, 8, 512, 1792], P('stage', 'expert')
- output 5: bfloat16 [8, 8, 1792, 512], P('stage', 'expert')
All inputs are finite; a program needn't handle non-finite values.
Results may differ from a plain program's by a relative error of at most 0.0011.
Values are sent between devices in bfloat16 or wider.
A program may use at most 1 GiB of HBM per device.

v0:
```python
import functools

import jax
import jax.numpy as jnp
from jax import lax
from jax.experimental import pallas as pl
from jax.experimental.pallas import tpu as pltpu
from jax.sharding import PartitionSpec as P

BF16 = jnp.bfloat16
F32 = jnp.float32
MESH = pl.DeviceIdType.MESH
TILE = 256
PARTS = 4
EARLY = 2
A, B, A_FAR, B_FAR = range(4)


def dot(lhs, rhs, lc=1, rc=0):
    return lax.dot_general(lhs, rhs, (((lc,), (rc,)), ((), ())), preferred_element_type=F32)


def routing(mb, num_loc, ids, gates, pos, gate_rows, pos_cols):
    first = lax.axis_index('expert') * num_loc
    tokens = ids.shape[-1]
    rows = 4 * num_loc
    lane = lax.broadcasted_iota(jnp.int32, (rows, tokens), 1)
    sub = lax.broadcasted_iota(jnp.int32, (rows, tokens), 0)
    expert = first + sub % num_loc

    def field(ref, k):
        return jnp.concatenate([ref[s, mb, k:k + 1, :] for s in range(4) for _ in range(num_loc)], axis=0)

    hit0, hit1 = field(ids, 0) == expert, field(ids, 1) == expert
    gate_rows[mb] = jnp.where(hit0, field(gates, 0), 0.0) + jnp.where(hit1, field(gates, 1), 0.0)
    taken = jnp.where(hit0 | hit1, 1, 0)
    run = taken
    step = 1
    while step < tokens:
        run = run + jnp.where(lane >= step, pltpu.roll(run, step, 1), 0)
        step *= 2
    slot = jnp.where(taken == 1, run - 1, -1)
    pos[mb] = slot
    pos_cols[mb, :, 0:rows] = slot.T


def pick(pos, gate_rows, mb, row, cap):
    tokens = pos.shape[-1]
    hit = pos[mb, pl.ds(row, 1), :] == lax.broadcasted_iota(jnp.int32, (cap, tokens), 0)
    gate = jnp.sum(jnp.where(hit, gate_rows[mb, pl.ds(row, 1), :], 0.0), axis=1, keepdims=True)
    return jnp.where(hit, 1.0, 0.0).astype(BF16), gate


def to_tokens(pos_cols, mb, block, rows, out, done):
    num_loc, cap, _ = rows.shape
    part = out.shape[2] // PARTS
    for m in range(PARTS):
        span = slice(m * part, (m + 1) * part)
        cols = pltpu.roll(pos_cols[mb, span, :], lax.rem(128 - num_loc * block, 128), 1)
        slot = lax.broadcasted_iota(jnp.int32, (part, cap), 1)
        sel = [jnp.where(cols[:, e:e + 1] == slot, 1.0, 0.0).astype(BF16) for e in range(num_loc)]
        total = dot(jnp.concatenate(sel, axis=1), rows[...].reshape(num_loc * cap, rows.shape[2]))
        out[mb, block, span, :] = total.astype(BF16)
        done(m)


def add_bf16(*refs):
    total = refs[0][...].astype(F32)
    for ref in refs[1:]:
        total += ref[...].astype(F32)
    return total.astype(BF16)


def stage_kernel(num_stages, cap, ids_in, gates_in, x_hbm, dy_hbm, win_hbm, wup_hbm, wout_hbm,
                 dx_hbm, y_hbm, yx_hbm, wide_hbm, tall_hbm,
                 ids, gates, xs, dys, win, wup, wout, pos, gate_rows, pos_cols, rows, ret, rin, cin,
                 wide_buf, tall_buf, q_early, u_early,
                 meta_send, meta_recv, hop_send, hop_recv, fwd_send, fwd_recv, dy_sem, dy_send, dy_recv,
                 ret_send, ret_recv, crs_send, crs_recv, w_sem, out_sem, res_sem, pace):
    stage, me = lax.axis_index('stage'), lax.axis_index('expert')
    nxt, prv = lax.rem(stage + 1, num_stages), lax.rem(stage + num_stages - 1, num_stages)
    core, chip = lax.rem(me, 2), me // 2
    other = 1 - core

    def peer(flip):
        new_core = other if flip % 2 else core
        new_chip = 1 - chip if flip // 2 else chip
        return 2 * new_chip + new_core

    partner, across = (stage, peer(1)), (stage, peer(2))
    num_loc, model, width = win.shape
    tokens = xs.shape[2]
    part = tokens // PARTS
    tiles = width // TILE

    def remote(src, dst, send, recv, device):
        return pltpu.make_async_remote_copy(src_ref=src, dst_ref=dst, send_sem=send, recv_sem=recv,
                                            device_id=device, device_id_type=MESH)

    def meta(flip, k, block=None):
        src, dst = ((ids_in, ids), (gates_in, gates))[k]
        block = 2 * (flip // 2) + core if block is None else block
        return remote(src, dst.at[block], meta_send.at[k, flip], meta_recv.at[k, block], (nxt, peer(flip)))

    def piece(mb, block, k):
        return xs.at[mb, block, pl.ds(k * part, part)]

    def hop(mb, k):
        src = x_hbm.at[mb, 0, pl.ds(k * part, part)]
        return remote(src, piece(mb, core, k), hop_send.at[mb, k], hop_recv.at[mb, k], (nxt, me))

    def near(mb, k, block=None):
        ref = piece(mb, core if block is None else block, k)
        return remote(ref, ref, fwd_send.at[mb, 0, k], fwd_recv.at[mb, 0, k], partner)

    def cross(mb, k):
        return remote(piece(mb, core, k), piece(mb, 2 + core, k), fwd_send.at[mb, 1, k], fwd_recv.at[mb, 1, k],
                      across)

    def far(mb, k, block=None):
        ref = piece(mb, 2 + core if block is None else block, k)
        return remote(ref, ref, fwd_send.at[mb, 2, k], fwd_recv.at[mb, 2, k], partner)

    def near_arrived(mb):
        for k in range(PARTS):
            near(mb, k, other).wait_recv()

    def far_arrived(mb):
        for k in range(PARTS):
            far(mb, k, 2 + other).wait_recv()

    dy_own = pltpu.make_async_copy(dy_hbm.at[0], dys.at[core], dy_sem)
    dy_near = remote(dy_hbm.at[0], dys.at[core], dy_send.at[0], dy_recv.at[0], partner)
    dy_near_in = remote(dy_hbm.at[0], dys.at[other], dy_send.at[0], dy_recv.at[0], partner)
    dy_cross = remote(dy_hbm.at[0], dys.at[2 + core], dy_send.at[1], dy_recv.at[1], across)
    dy_far = remote(dys.at[2 + core], dys.at[2 + core], dy_send.at[2], dy_recv.at[2], partner)
    dy_far_in = remote(dys.at[2 + other], dys.at[2 + other], dy_send.at[2], dy_recv.at[2], partner)

    def back(mb, k, m, block=None):
        rows_m = pl.ds(m * part, part)
        src = ret.at[mb, 2 * k + other if block is None else block, rows_m]
        return remote(src, rin.at[mb, k, rows_m], ret_send.at[mb, k, m], ret_recv.at[mb, k, m], partner)

    def back_arrived(mb, k):
        for m in range(PARTS):
            back(mb, k, m).wait_recv()

    def send_back(mb, block):
        def done(m):
            @pl.when(lax.rem(block, 2) != core)
            def _():
                back(mb, block // 2, m, block).start()
        return done

    dx_cross = remote(ret.at[0, 2 + core], cin, crs_send, crs_recv, across)

    def dx_across():
        back_arrived(0, 1)
        ret[0, 2 + core] = add_bf16(ret.at[0, 2 + core], rin.at[0, 1])
        dx_cross.start()

    dx_save = pltpu.make_async_copy(ret.at[0, core], dx_hbm, res_sem.at[0])
    y_save = pltpu.make_async_copy(ret.at[1, core], y_hbm, res_sem.at[1])
    yx_save = pltpu.make_async_copy(ret.at[1, 2 + core], yx_hbm, res_sem.at[2])

    weights = [pltpu.make_async_copy(src.at[0], dst, w_sem.at[k])
               for k, (src, dst) in enumerate(((win_hbm, win), (wup_hbm, wup), (wout_hbm, wout)))]

    def outs(st):
        slot = lax.rem(st, 2)
        block, e = st // num_loc, lax.rem(st, num_loc)
        span = pl.ds(pl.multiple_of(block * cap, cap), cap)
        return (pltpu.make_async_copy(wide_buf.at[slot], wide_hbm.at[e, :, :, span], out_sem.at[slot, 0]),
                pltpu.make_async_copy(tall_buf.at[slot], tall_hbm.at[e, :, :, span], out_sem.at[slot, 1]))

    def at(now, when, on_core=None):
        cond = now == when if on_core is None else (now == when) & (core == on_core)
        return pl.when(cond)

    barrier = pltpu.get_barrier_semaphore()
    for device in [(prv, peer(flip)) for flip in range(4)] + [partner, across]:
        pl.semaphore_signal(barrier, inc=1, device_id=device, device_id_type=MESH)
    pl.semaphore_wait(barrier, 6)

    for flip in range(4):
        for k in range(2):
            meta(flip, k).start()

    @pl.when(core == 0)
    def _():
        for k in range(PARTS):
            hop(0, k).start()
        dy_cross.start()

    dy_near.start()
    dy_own.start()
    for copy in weights:
        copy.start()

    for block in range(4):
        for k in range(2):
            meta(0, k, block).wait_recv()
    for mb in range(2):
        routing(mb, num_loc, ids, gates, pos, gate_rows, pos_cols)
    dy_own.wait()
    dy_near_in.wait_recv()
    for copy in weights:
        copy.wait()

    def cotangent(st):
        sel, gate = pick(pos, gate_rows, 0, st, cap)
        return sel, gate * dot(sel, dys[st // num_loc])

    def early_step(st, carry):
        q = cotangent(st)[1].astype(BF16)
        q_early[st] = q
        for t in range(tiles):
            cols = slice(t * TILE, (t + 1) * TILE)
            u_early[st, :, cols] = dot(q, wout[lax.rem(st, num_loc), cols, :], 1, 1)
        return carry

    lax.fori_loop(0, EARLY, early_step, 0)

    @pl.when(core == 0)
    def _():
        for k in range(PARTS):
            hop(0, k).wait_recv()
            near(0, k).start()
            cross(0, k).start()
            if k == PARTS - 2:
                pl.semaphore_signal(pace, inc=1, device_id=partner, device_id_type=MESH)

    @pl.when(core == 1)
    def _():
        pl.semaphore_wait(pace, 1)
        for k in range(PARTS):
            hop(0, k).start()
        dy_cross.start()
        near_arrived(0)

    steps = 4 * num_loc
    half, most = PARTS // 2, PARTS - 1

    def pass_on(mb, lo, hi):
        for k in range(lo, hi):
            hop(mb, k).wait_recv()
            near(mb, k).start()
            cross(mb, k).start()

    def pass_far(mb, lo, hi):
        for k in range(lo, hi):
            cross(mb, k).wait_recv()
            far(mb, k).start()

    def backward_step(early, st, carry):
        block, e = st // num_loc, lax.rem(st, num_loc)
        slot = lax.rem(st, 2)

        @at(st, 1, on_core=1)
        def _():
            pass_on(0, 0, most)

        @at(st, num_loc, on_core=1)
        def _():
            pass_on(0, most, PARTS)

        @at(st, num_loc, on_core=0)
        def _():
            for k in range(PARTS):
                hop(1, k).start()
            near_arrived(0)

        @at(st, num_loc + 1, on_core=0)
        def _():
            dy_cross.wait_recv()
            dy_far.start()
            pass_far(0, 0, PARTS)

        @at(st, 2 * num_loc, on_core=0)
        def _():
            pass_on(1, 0, half)

        @at(st, 2 * num_loc, on_core=1)
        def _():
            for k in range(PARTS):
                hop(1, k).start()
            far_arrived(0)
            dy_far_in.wait_recv()

        @at(st, 2 * num_loc + 1, on_core=0)
        def _():
            pass_on(1, half, PARTS)

        @at(st, 2 * num_loc + 1, on_core=1)
        def _():
            dy_cross.wait_recv()
            dy_far.start()
            pass_far(0, 0, most)

        @at(st, 3 * num_loc, on_core=1)
        def _():
            pass_far(0, most, PARTS)
            pass_on(1, 0, half)

        @at(st, 3 * num_loc, on_core=0)
        def _():
            far_arrived(0)
            dy_far_in.wait_recv()

        @at(st, 3 * num_loc + 1, on_core=1)
        def _():
            pass_on(1, half, PARTS)

        @at(st, 3 * num_loc + 1, on_core=0)
        def _():
            dx_across()

        @pl.when(st >= 2)
        def _():
            for copy in outs(st - 2):
                copy.wait()

        if early:
            sel = pick(pos, gate_rows, 0, st, cap)[0]
            gdy = q_early[st].astype(F32)
        else:
            sel, gdy = cotangent(st)
        x = dot(sel, xs[0, block])
        tall_buf[slot, 0] = x.T.astype(BF16)
        tall_buf[slot, 1] = gdy.T.astype(BF16)
        x, q = x.astype(BF16), gdy.astype(BF16)
        for t in range(tiles):
            cols = slice(t * TILE, (t + 1) * TILE)
            a = dot(x, win[e, :, cols])
            b = dot(x, wup[e, :, cols])
            u = u_early[st, :, cols] if early else dot(q, wout[e, cols, :], 1, 1)
            sig = jax.nn.sigmoid(a)
            act = a * sig
            wide_buf[slot, t, 0] = (u * b * sig * (1.0 + a * (1.0 - sig))).astype(BF16)
            wide_buf[slot, t, 1] = (u * act).astype(BF16)
            wide_buf[slot, t, 2] = (act * b).astype(BF16)
        g_in = jnp.concatenate([wide_buf[slot, t, 0] for t in range(tiles)], axis=1)
        g_up = jnp.concatenate([wide_buf[slot, t, 1] for t in range(tiles)], axis=1)
        rows[e] = (dot(g_in, win[e], 1, 1) + dot(g_up, wup[e], 1, 1)).astype(BF16)
        for copy in outs(st):
            copy.start()

        @pl.when(e == num_loc - 1)
        def _():
            to_tokens(pos_cols, 0, block, rows, ret, send_back(0, block))

        return carry

    lax.fori_loop(0, EARLY, functools.partial(backward_step, True), 0)
    lax.fori_loop(EARLY, steps, functools.partial(backward_step, False), 0)
    for st in (steps - 2, steps - 1):
        for copy in outs(st):
            copy.wait()

    def forward_step(st, carry):
        block, e = st // num_loc, lax.rem(st, num_loc)

        @at(st, 0, on_core=1)
        def _():
            near_arrived(1)

        @at(st, 1, on_core=1)
        def _():
            dx_across()

        @at(st, num_loc, on_core=0)
        def _():
            near_arrived(1)

        @at(st, num_loc + 1, on_core=0)
        def _():
            pass_far(1, 0, PARTS)

        @at(st, 2 * num_loc, on_core=1)
        def _():
            far_arrived(1)

        @at(st, 2 * num_loc + 1, on_core=1)
        def _():
            pass_far(1, 0, most)

        @at(st, 3 * num_loc, on_core=1)
        def _():
            pass_far(1, most, PARTS)

        @at(st, 3 * num_loc)
        def _():
            back_arrived(1, 0)
            ret[1, core] = add_bf16(ret.at[1, core], rin.at[1, 0])
            y_save.start()

        @at(st, 3 * num_loc, on_core=0)
        def _():
            far_arrived(1)

        sel, gate = pick(pos, gate_rows, 1, st, cap)
        x = dot(sel, xs[1, block]).astype(BF16)
        for t in range(tiles):
            cols = slice(t * TILE, (t + 1) * TILE)
            a = dot(x, win[e, :, cols])
            b = dot(x, wup[e, :, cols])
            wide_buf[0, t, 0] = (a * jax.nn.sigmoid(a) * b).astype(BF16)
        hid = jnp.concatenate([wide_buf[0, t, 0] for t in range(tiles)], axis=1)
        rows[e] = (gate * dot(hid, wout[e])).astype(BF16)

        @pl.when(e == num_loc - 1)
        def _():
            to_tokens(pos_cols, 1, block, rows, ret, send_back(1, block))

        return carry

    lax.fori_loop(0, steps, forward_step, 0)
    back_arrived(1, 1)
    ret[1, 2 + core] = add_bf16(ret.at[1, 2 + core], rin.at[1, 1])
    yx_save.start()
    back_arrived(0, 0)
    dx_cross.wait_recv()
    ret[0, core] = add_bf16(ret.at[0, core], rin.at[0, 0], cin)
    dx_save.start()

    for flip in range(4):
        for k in range(2):
            meta(flip, k).wait_send()
    for mb in range(2):
        for k in range(PARTS):
            hop(mb, k).wait_send()
            near(mb, k).wait_send()
            cross(mb, k).wait_send()
            far(mb, k).wait_send()
            for j in range(2):
                back(mb, j, k).wait_send()
    for copy in (dy_near, dy_cross, dy_far, dx_cross):
        copy.wait_send()
    for copy in (y_save, yx_save, dx_save):
        copy.wait()


def stage_call(num_stages, cap, ids, gates, x_acts, d_out, w_in, w_up, w_out):
    _, num_loc, model, width = w_in.shape
    tokens = x_acts.shape[2]
    slots = 4 * cap
    whole = pl.BlockSpec(memory_space=pltpu.VMEM)
    anyspace = pl.BlockSpec(memory_space=pl.ANY)
    block = jax.ShapeDtypeStruct((tokens, model), BF16)
    wide = jax.ShapeDtypeStruct((num_loc, width // TILE, 3, slots, TILE), BF16)
    tall = jax.ShapeDtypeStruct((num_loc, 2, model, slots), BF16)
    vmem = pltpu.VMEM
    dma = pltpu.SemaphoreType.DMA
    return pl.pallas_call(
        functools.partial(stage_kernel, num_stages, cap),
        out_shape=[block] * 3 + [wide, tall],
        in_specs=[whole] * 2 + [anyspace] * 5,
        out_specs=[anyspace] * 5,
        scratch_shapes=[
            vmem((4,) + ids.shape, jnp.int32), vmem((4,) + gates.shape, F32),
            vmem((2, 4, tokens, model), BF16), vmem((4, tokens, model), BF16),
            vmem((num_loc, model, width), BF16), vmem((num_loc, model, width), BF16),
            vmem((num_loc, width, model), BF16),
            vmem((2, 4 * num_loc, tokens), jnp.int32), vmem((2, 4 * num_loc, tokens), F32),
            vmem((2, tokens, 128), jnp.int32),
            vmem((num_loc, cap, model), BF16), vmem((2, 4, tokens, model), BF16),
            vmem((2, 2, tokens, model), BF16), vmem((tokens, model), BF16),
            vmem((2, width // TILE, 3, cap, TILE), BF16), vmem((2, 2, model, cap), BF16),
            vmem((EARLY, cap, model), BF16), vmem((EARLY, cap, width), F32),
            dma((2, 4)), dma((2, 4)), dma((2, PARTS)), dma((2, PARTS)), dma((2, 3, PARTS)), dma((2, 3, PARTS)),
            dma, dma((3,)), dma((3,)), dma((2, 2, PARTS)), dma((2, 2, PARTS)), dma, dma, dma((3,)), dma((2, 2)), dma((3,)),
            pltpu.SemaphoreType.REGULAR,
        ],
        compiler_params=pltpu.CompilerParams(collective_id=0, has_side_effects=True, vmem_limit_bytes=66_500_000),
        cost_estimate=pl.CostEstimate(flops=16 * num_loc * slots * model * width,
                                      bytes_accessed=70 * 2 ** 20, transcendentals=0),
        name='stage_layer',
    )(ids, gates, x_acts, d_out, w_in, w_up, w_out)


def weight_kernel(tall, wide, din_ref, dup_ref, dout_ref):
    for e in range(tall.shape[0]):
        din_ref[e] = dot(tall[e, 0], wide[e, 0, 0]).astype(BF16)
        dup_ref[e] = dot(tall[e, 0], wide[e, 0, 1]).astype(BF16)
        dout_ref[e] = dot(tall[e, 1], wide[e, 0, 2]).T.astype(BF16)


def weight_call(wide, tall):
    num_loc, tiles, _, slots, _ = wide.shape
    model, width = tall.shape[2], tiles * TILE
    return pl.pallas_call(
        weight_kernel,
        grid=(tiles,),
        in_specs=[pl.BlockSpec(tall.shape, lambda t: (0, 0, 0, 0)),
                  pl.BlockSpec((num_loc, 1, 3, slots, TILE), lambda t: (0, t, 0, 0, 0))],
        out_specs=[pl.BlockSpec((num_loc, model, TILE), lambda t: (0, 0, t))] * 2
        + [pl.BlockSpec((num_loc, TILE, model), lambda t: (0, t, 0))],
        out_shape=[jax.ShapeDtypeStruct((num_loc, model, width), BF16)] * 2
        + [jax.ShapeDtypeStruct((num_loc, width, model), BF16)],
        compiler_params=pltpu.CompilerParams(dimension_semantics=('arbitrary',)),
        cost_estimate=pl.CostEstimate(flops=6 * num_loc * slots * model * width,
                                      bytes_accessed=50 * 2 ** 20, transcendentals=0),
        name='weight_grads',
    )(tall, wide)


def solution(mesh):
    group = mesh.shape['expert']
    stages = mesh.shape['stage']

    def device_fn(x_acts, expert_ids, gate_wts, w_in, w_up, w_out, d_out):
        num_loc = w_in.shape[1]
        tokens = x_acts.shape[2]
        top_k = expert_ids.shape[3]
        cap = 3 * top_k * tokens // (2 * num_loc * group)
        ids = jnp.swapaxes(expert_ids[:, 0], 1, 2)
        gates = jnp.swapaxes(gate_wts[:, 0], 1, 2)
        dx_home, y_loc, y_x, wide, tall = stage_call(
            stages, cap, ids, gates, x_acts, d_out, w_in, w_up, w_out)
        d_x = lax.ppermute(dx_home, 'stage', [((s + 1) % stages, s) for s in range(stages)])
        y_in = lax.ppermute(y_x, 'expert', [(i, i ^ 2) for i in range(group)])
        d_in, d_up, d_wout = weight_call(wide, tall)
        y = (y_loc.astype(F32) + y_in.astype(F32)).astype(BF16)
        return y[None], d_x[None], d_in[None], d_up[None], d_wout[None]

    tok_spec = P(None, 'stage', 'expert', None)
    w_spec = P('stage', 'expert', None, None)
    row_spec = P('stage', 'expert', None)
    return jax.shard_map(device_fn, mesh=mesh,
                         in_specs=(tok_spec, tok_spec, tok_spec, w_spec, w_spec, w_spec, row_spec),
                         out_specs=(row_spec, row_spec, w_spec, w_spec, w_spec), check_vma=False)
```

profile of v0, /device:TPU:1, one launch (start us, length us, event | category | flops | bytes accessed | tf_op | source)
XLA Modules:
  0.0 140.7 jit_solution(3175473982614657593)
XLA Ops:
  0.6 110.9 %stage_layer.1 = (bf16[1024,512]{1,0:T(8,128)(2,1)}, bf16[1024,512]{1,0:T(8,128)(2,1)}, bf16[1024,512]{1,0:T(8,128)(2,1)}, bf16[2,7,3,1536,256]{4,3,2,1,0:T(8,128)(2,1)}, bf16[2,2,512,1536]{3,2,1,0:T(8,128)(2,1)}) custom-call(s32[2,2,1024]{2,1,0:T(2,128)} %bitcast.13, f32[2,2,1024]{2,1,0:T(2,128)} %bitcast.14, bf16[2,1,1024,512]{3,2,1,0:T(8,128)(2,1)} %x_hbm.1, ...), custom_call_target="tpu_custom_call" | custom-call | flops 45097156608 | bytes 73400320 | tf_op jit(solution)/shard_map/stage_layer/pallas_call | solution.py:454
  111.5 2.1 %collective-permute-start = (bf16[1024,512]{1,0:T(8,128)(2,1)}, bf16[1024,512]{1,0:T(8,128)(2,1)S(1)}, u32[]{:S(2)}, u32[]{:S(2)}) collective-permute-start(bf16[1024,512]{1,0:T(8,128)(2,1)} %get-tuple-element.14), channel_id=1, source_target_pairs={{0,2},{1,3},{2,0},{3,1},{4,6},{5,7},{6,4},{7,5},{8,10},{9,11},{10,... | collective-permute-start | bytes 3145736 | tf_op jit(solution)/shard_map/ppermute | solution.py:521
  113.6 0.8 collective-permute-start.1
  114.3 0.0 copy-start
  114.3 24.1 %weight_grads.1 = (bf16[2,512,1792]{2,1,0:T(8,128)(2,1)}, bf16[2,512,1792]{2,1,0:T(8,128)(2,1)}, bf16[2,1792,512]{2,1,0:T(8,128)(2,1)}) custom-call(bf16[2,2,512,1536]{3,2,1,0:T(8,128)(2,1)} %get-tuple-element.16.tall, bf16[2,7,3,1536,256]{4,3,2,1,0:T(8,128)(2,1)} %get-tuple-element.17.wide), custom_call_target="tpu_custom_call" | custom-call | flops 16911433728 | bytes 52428800 | tf_op jit(solution)/shard_map/weight_grads/pallas_call | solution.py:491
  138.4 0.0 collective-permute-done.1
  138.4 0.0 collective-permute-done
  138.4 0.0 copy-done
  138.4 1.3 fusion
  139.7 1.0 copy.13
Async XLA Ops:
  111.5 26.9 %collective-permute-start = (bf16[1024,512]{1,0:T(8,128)(2,1)}, bf16[1024,512]{1,0:T(8,128)(2,1)S(1)}, u32[]{:S(2)}, u32[]{:S(2)}) collective-permute-start(bf16[1024,512]{1,0:T(8,128)(2,1)} %get-tuple-element.14), channel_id=1, source_target_pairs={{0,2},{1,3},{2,0},{3,1},{4,6},{5,7},{6,4},{7,5},{8,10},{9,11},{10,... | collective-permute-start | bytes 3145736 | tf_op jit(solution)/shard_map/ppermute | solution.py:521
  113.6 24.8 %collective-permute-start.1 = (bf16[1024,512]{1,0:T(8,128)(2,1)}, bf16[1024,512]{1,0:T(8,128)(2,1)S(1)}, u32[]{:S(2)}, u32[]{:S(2)}) collective-permute-start(bf16[1024,512]{1,0:T(8,128)(2,1)} %get-tuple-element.15), channel_id=1, source_target_pairs={{4,0},{8,4},{12,8},{16,12},{20,16},{24,20},{28,24},{0,28},{5,1},{9... | collective-permute-start | bytes 3145736 | tf_op jit(solution)/shard_map/ppermute | solution.py:520
  114.3 24.1 %copy-start = (bf16[1024,512]{1,0:T(8,128)(2,1)S(1)}, bf16[1024,512]{1,0:T(8,128)(2,1)}, u32[]{:S(2)}) copy-start(bf16[1024,512]{1,0:T(8,128)(2,1)} %get-tuple-element.13) | copy-start | bytes 3145732
where the time goes:
time: 141 us
  Pallas kernels  135 us (96%)
  starting transfers between devices  2.8 us (2%)
    pallas_call x1, Pallas kernels, stage_call(): pl.pallas_call(functools.partial(stage_kernel, num_stages, cap), out_shap...  111 us
    pallas_call x1, Pallas kernels, weight_call(): pl.pallas_call(weight_kernel, grid=(tiles,), in_specs=[pl.BlockSpec(tall....  24.1 us
  transfers between devices with their start and end apart: 2, of which 0 were waited for; matrix products, arithmetic and copies ran while one was open for 0% of the time, Pallas kernels for 17%

commit v1 on v0

--- a/solution.py
+++ b/solution.py
@@ -51,7 +51,7 @@
     return jnp.where(hit, 1.0, 0.0).astype(BF16), gate
 
 
-def to_tokens(pos_cols, mb, block, rows, out, done):
+def to_tokens(pos_cols, mb, block, rows, out):
     num_loc, cap, _ = rows.shape
     part = out.shape[2] // PARTS
     for m in range(PARTS):
@@ -61,7 +61,6 @@
         sel = [jnp.where(cols[:, e:e + 1] == slot, 1.0, 0.0).astype(BF16) for e in range(num_loc)]
         total = dot(jnp.concatenate(sel, axis=1), rows[...].reshape(num_loc * cap, rows.shape[2]))
         out[mb, block, span, :] = total.astype(BF16)
-        done(m)
 
 
 def add_bf16(*refs):
@@ -136,26 +135,19 @@
     dy_far = remote(dys.at[2 + core], dys.at[2 + core], dy_send.at[2], dy_recv.at[2], partner)
     dy_far_in = remote(dys.at[2 + other], dys.at[2 + other], dy_send.at[2], dy_recv.at[2], partner)
 
-    def back(mb, k, m, block=None):
-        rows_m = pl.ds(m * part, part)
-        src = ret.at[mb, 2 * k + other if block is None else block, rows_m]
-        return remote(src, rin.at[mb, k, rows_m], ret_send.at[mb, k, m], ret_recv.at[mb, k, m], partner)
-
-    def back_arrived(mb, k):
-        for m in range(PARTS):
-            back(mb, k, m).wait_recv()
+    def back(mb, k, block=None):
+        src = ret.at[mb, 2 * k + other if block is None else block]
+        return remote(src, rin.at[mb, k], ret_send.at[mb, k], ret_recv.at[mb, k], partner)
 
     def send_back(mb, block):
-        def done(m):
-            @pl.when(lax.rem(block, 2) != core)
-            def _():
-                back(mb, block // 2, m, block).start()
-        return done
+        @pl.when(lax.rem(block, 2) != core)
+        def _():
+            back(mb, block // 2, block).start()
 
     dx_cross = remote(ret.at[0, 2 + core], cin, crs_send, crs_recv, across)
 
     def dx_across():
-        back_arrived(0, 1)
+        back(0, 1).wait_recv()
         ret[0, 2 + core] = add_bf16(ret.at[0, 2 + core], rin.at[0, 1])
         dx_cross.start()
 
@@ -347,7 +339,8 @@
 
         @pl.when(e == num_loc - 1)
         def _():
-            to_tokens(pos_cols, 0, block, rows, ret, send_back(0, block))
+            to_tokens(pos_cols, 0, block, rows, ret)
+            send_back(0, block)
 
         return carry
 
@@ -390,7 +383,7 @@
 
         @at(st, 3 * num_loc)
         def _():
-            back_arrived(1, 0)
+            back(1, 0).wait_recv()
             ret[1, core] = add_bf16(ret.at[1, core], rin.at[1, 0])
             y_save.start()
 
@@ -410,15 +403,16 @@
 
         @pl.when(e == num_loc - 1)
         def _():
-            to_tokens(pos_cols, 1, block, rows, ret, send_back(1, block))
+            to_tokens(pos_cols, 1, block, rows, ret)
+            send_back(1, block)
 
         return carry
 
     lax.fori_loop(0, steps, forward_step, 0)
-    back_arrived(1, 1)
+    back(1, 1).wait_recv()
     ret[1, 2 + core] = add_bf16(ret.at[1, 2 + core], rin.at[1, 1])
     yx_save.start()
-    back_arrived(0, 0)
+    back(0, 0).wait_recv()
     dx_cross.wait_recv()
     ret[0, core] = add_bf16(ret.at[0, core], rin.at[0, 0], cin)
     dx_save.start()
@@ -432,8 +426,8 @@
             near(mb, k).wait_send()
             cross(mb, k).wait_send()
             far(mb, k).wait_send()
-            for j in range(2):
-                back(mb, j, k).wait_send()
+        for k in range(2):
+            back(mb, k).wait_send()
     for copy in (dy_near, dy_cross, dy_far, dx_cross):
         copy.wait_send()
     for copy in (y_save, yx_save, dx_save):
@@ -468,7 +462,7 @@
             vmem((2, width // TILE, 3, cap, TILE), BF16), vmem((2, 2, model, cap), BF16),
             vmem((EARLY, cap, model), BF16), vmem((EARLY, cap, width), F32),
             dma((2, 4)), dma((2, 4)), dma((2, PARTS)), dma((2, PARTS)), dma((2, 3, PARTS)), dma((2, 3, PARTS)),
-            dma, dma((3,)), dma((3,)), dma((2, 2, PARTS)), dma((2, 2, PARTS)), dma, dma, dma((3,)), dma((2, 2)), dma((3,)),
+            dma, dma((3,)), dma((3,)), dma((2, 2)), dma((2, 2)), dma, dma, dma((3,)), dma((2, 2)), dma((3,)),
             pltpu.SemaphoreType.REGULAR,
         ],
         compiler_params=pltpu.CompilerParams(collective_id=0, has_side_effects=True, vmem_limit_bytes=66_500_000),

time: 141 us -> 138 us (0.979)
  Pallas kernels: 135 us -> 132 us
    pallas_call x1, Pallas kernels: 111 us -> 108 us  [stage_call(): pl.pallas_call(functools.partial(stage_kernel, num_stages, cap), out_shap...]
  transfers between devices with their start and end apart: 2 -> 2, of which waited for: 0 -> 0; matrix products, arithmetic and copies ran while one was open for 0% -> 0% of each run, Pallas kernels for 17% -> 18%
where the time goes in v1:
time: 138 us; the launch traced here: 137 us
  Pallas kernels  132 us (96%)
  starting transfers between devices  2.82 us (2%)
    pallas_call x1, Pallas kernels, stage_call(): pl.pallas_call(functools.partial(stage_kernel, num_stages, cap), out_shap...  108 us
    pallas_call x1, Pallas kernels, weight_call(): pl.pallas_call(weight_kernel, grid=(tiles,), in_specs=[pl.BlockSpec(tall....  24.1 us
  transfers between devices with their start and end apart: 2, of which 0 were waited for; matrix products, arithmetic and copies ran while one was open for 0% of the time, Pallas kernels for 18%

profile of v1, /device:TPU:1, one launch (start us, length us, event | category | flops | bytes accessed | tf_op | source)
XLA Modules:
  0.0 137.4 jit_solution(12646687166271619194)
XLA Ops:
  0.6 107.6 %stage_layer.1 = (bf16[1024,512]{1,0:T(8,128)(2,1)}, bf16[1024,512]{1,0:T(8,128)(2,1)}, bf16[1024,512]{1,0:T(8,128)(2,1)}, bf16[2,7,3,1536,256]{4,3,2,1,0:T(8,128)(2,1)}, bf16[2,2,512,1536]{3,2,1,0:T(8,128)(2,1)}) custom-call(s32[2,2,1024]{2,1,0:T(2,128)} %bitcast.13, f32[2,2,1024]{2,1,0:T(2,128)} %bitcast.14, bf16[2,1,1024,512]{3,2,1,0:T(8,128)(2,1)} %x_hbm.1, ...), custom_call_target="tpu_custom_call" | custom-call | flops 45097156608 | bytes 73400320 | tf_op jit(solution)/shard_map/stage_layer/pallas_call | solution.py:448
  108.3 2.1 %collective-permute-start = (bf16[1024,512]{1,0:T(8,128)(2,1)}, bf16[1024,512]{1,0:T(8,128)(2,1)S(1)}, u32[]{:S(2)}, u32[]{:S(2)}) collective-permute-start(bf16[1024,512]{1,0:T(8,128)(2,1)} %get-tuple-element.14), channel_id=1, source_target_pairs={{0,2},{1,3},{2,0},{3,1},{4,6},{5,7},{6,4},{7,5},{8,10},{9,11},{10,... | collective-permute-start | bytes 3145736 | tf_op jit(solution)/shard_map/ppermute | solution.py:515
  110.3 0.8 collective-permute-start.1
  111.1 0.0 copy-start
  111.1 24.1 %weight_grads.1 = (bf16[2,512,1792]{2,1,0:T(8,128)(2,1)}, bf16[2,512,1792]{2,1,0:T(8,128)(2,1)}, bf16[2,1792,512]{2,1,0:T(8,128)(2,1)}) custom-call(bf16[2,2,512,1536]{3,2,1,0:T(8,128)(2,1)} %get-tuple-element.16.tall, bf16[2,7,3,1536,256]{4,3,2,1,0:T(8,128)(2,1)} %get-tuple-element.17.wide), custom_call_target="tpu_custom_call" | custom-call | flops 16911433728 | bytes 52428800 | tf_op jit(solution)/shard_map/weight_grads/pallas_call | solution.py:485
  135.2 0.0 collective-permute-done.1
  135.2 0.0 collective-permute-done
  135.2 0.0 copy-done
  135.2 1.3 fusion
  136.4 1.0 copy.13
Async XLA Ops:
  108.3 26.9 %collective-permute-start = (bf16[1024,512]{1,0:T(8,128)(2,1)}, bf16[1024,512]{1,0:T(8,128)(2,1)S(1)}, u32[]{:S(2)}, u32[]{:S(2)}) collective-permute-start(bf16[1024,512]{1,0:T(8,128)(2,1)} %get-tuple-element.14), channel_id=1, source_target_pairs={{0,2},{1,3},{2,0},{3,1},{4,6},{5,7},{6,4},{7,5},{8,10},{9,11},{10,... | collective-permute-start | bytes 3145736 | tf_op jit(solution)/shard_map/ppermute | solution.py:515
  110.3 24.8 %collective-permute-start.1 = (bf16[1024,512]{1,0:T(8,128)(2,1)}, bf16[1024,512]{1,0:T(8,128)(2,1)S(1)}, u32[]{:S(2)}, u32[]{:S(2)}) collective-permute-start(bf16[1024,512]{1,0:T(8,128)(2,1)} %get-tuple-element.15), channel_id=1, source_target_pairs={{4,0},{8,4},{12,8},{16,12},{20,16},{24,20},{28,24},{0,28},{5,1},{9... | collective-permute-start | bytes 3145736 | tf_op jit(solution)/shard_map/ppermute | solution.py:514
  111.1 24.1 %copy-start = (bf16[1024,512]{1,0:T(8,128)(2,1)S(1)}, bf16[1024,512]{1,0:T(8,128)(2,1)}, u32[]{:S(2)}) copy-start(bf16[1024,512]{1,0:T(8,128)(2,1)} %get-tuple-element.13) | copy-start | bytes 3145732

commit v2 on v1

--- a/solution.py
+++ b/solution.py
@@ -227,7 +227,6 @@
         pl.semaphore_wait(pace, 1)
         for k in range(PARTS):
             hop(0, k).start()
-        dy_cross.start()
         near_arrived(0)
 
     steps = 4 * num_loc
@@ -250,6 +249,7 @@
 
         @at(st, 1, on_core=1)
         def _():
+            dy_cross.start()
             pass_on(0, 0, most)
 
         @at(st, num_loc, on_core=1)
@@ -267,10 +267,6 @@
             dy_cross.wait_recv()
             dy_far.start()
             pass_far(0, 0, PARTS)
-
-        @at(st, 2 * num_loc, on_core=0)
-        def _():
-            pass_on(1, 0, half)
 
         @at(st, 2 * num_loc, on_core=1)
         def _():
@@ -281,17 +277,17 @@
 
         @at(st, 2 * num_loc + 1, on_core=0)
         def _():
-            pass_on(1, half, PARTS)
+            pass_on(1, 0, PARTS)
 
         @at(st, 2 * num_loc + 1, on_core=1)
         def _():
             dy_cross.wait_recv()
             dy_far.start()
-            pass_far(0, 0, most)
+            pass_far(0, 0, half)
 
         @at(st, 3 * num_loc, on_core=1)
         def _():
-            pass_far(0, most, PARTS)
+            pass_far(0, half, PARTS)
             pass_on(1, 0, half)
 
         @at(st, 3 * num_loc, on_core=0)

time: 138 us -> 138 us (level)
  transfers between devices with their start and end apart: 2 -> 2, of which waited for: 0 -> 0; matrix products, arithmetic and copies ran while one was open for 0% -> 0% of each run, Pallas kernels for 18% -> 17%
where the time goes in v2:
time: 138 us
  Pallas kernels  132 us (96%)
  starting transfers between devices  2.82 us (2%)
    pallas_call x1, Pallas kernels, stage_call(): pl.pallas_call(functools.partial(stage_kernel, num_stages, cap), out_shap...  108 us
    pallas_call x1, Pallas kernels, weight_call(): pl.pallas_call(weight_kernel, grid=(tiles,), in_specs=[pl.BlockSpec(tall....  24.1 us
  transfers between devices with their start and end apart: 2, of which 0 were waited for; matrix products, arithmetic and copies ran while one was open for 0% of the time, Pallas kernels for 17%

profile of v2, /device:TPU:1, one launch (start us, length us, event | category | flops | bytes accessed | tf_op | source)
XLA Modules:
  0.0 137.8 jit_solution(15156617101809116151)
XLA Ops:
  0.6 108.0 %stage_layer.1 = (bf16[1024,512]{1,0:T(8,128)(2,1)}, bf16[1024,512]{1,0:T(8,128)(2,1)}, bf16[1024,512]{1,0:T(8,128)(2,1)}, bf16[2,7,3,1536,256]{4,3,2,1,0:T(8,128)(2,1)}, bf16[2,2,512,1536]{3,2,1,0:T(8,128)(2,1)}) custom-call(s32[2,2,1024]{2,1,0:T(2,128)} %bitcast.13, f32[2,2,1024]{2,1,0:T(2,128)} %bitcast.14, bf16[2,1,1024,512]{3,2,1,0:T(8,128)(2,1)} %x_hbm.1, ...), custom_call_target="tpu_custom_call" | custom-call | flops 45097156608 | bytes 73400320 | tf_op jit(solution)/shard_map/stage_layer/pallas_call | solution.py:444
  108.6 2.1 %collective-permute-start = (bf16[1024,512]{1,0:T(8,128)(2,1)}, bf16[1024,512]{1,0:T(8,128)(2,1)S(1)}, u32[]{:S(2)}, u32[]{:S(2)}) collective-permute-start(bf16[1024,512]{1,0:T(8,128)(2,1)} %get-tuple-element.14), channel_id=1, source_target_pairs={{0,2},{1,3},{2,0},{3,1},{4,6},{5,7},{6,4},{7,5},{8,10},{9,11},{10,... | collective-permute-start | bytes 3145736 | tf_op jit(solution)/shard_map/ppermute | solution.py:511
  110.7 0.8 collective-permute-start.1
  111.4 0.0 copy-start
  111.5 24.1 %weight_grads.1 = (bf16[2,512,1792]{2,1,0:T(8,128)(2,1)}, bf16[2,512,1792]{2,1,0:T(8,128)(2,1)}, bf16[2,1792,512]{2,1,0:T(8,128)(2,1)}) custom-call(bf16[2,2,512,1536]{3,2,1,0:T(8,128)(2,1)} %get-tuple-element.16.tall, bf16[2,7,3,1536,256]{4,3,2,1,0:T(8,128)(2,1)} %get-tuple-element.17.wide), custom_call_target="tpu_custom_call" | custom-call | flops 16911433728 | bytes 52428800 | tf_op jit(solution)/shard_map/weight_grads/pallas_call | solution.py:481
  135.5 0.0 collective-permute-done.1
  135.5 0.0 collective-permute-done
  135.5 0.0 copy-done
  135.5 1.3 fusion
  136.8 1.0 copy.13
Async XLA Ops:
  108.6 26.9 %collective-permute-start = (bf16[1024,512]{1,0:T(8,128)(2,1)}, bf16[1024,512]{1,0:T(8,128)(2,1)S(1)}, u32[]{:S(2)}, u32[]{:S(2)}) collective-permute-start(bf16[1024,512]{1,0:T(8,128)(2,1)} %get-tuple-element.14), channel_id=1, source_target_pairs={{0,2},{1,3},{2,0},{3,1},{4,6},{5,7},{6,4},{7,5},{8,10},{9,11},{10,... | collective-permute-start | bytes 3145736 | tf_op jit(solution)/shard_map/ppermute | solution.py:511
  110.7 24.8 %collective-permute-start.1 = (bf16[1024,512]{1,0:T(8,128)(2,1)}, bf16[1024,512]{1,0:T(8,128)(2,1)S(1)}, u32[]{:S(2)}, u32[]{:S(2)}) collective-permute-start(bf16[1024,512]{1,0:T(8,128)(2,1)} %get-tuple-element.15), channel_id=1, source_target_pairs={{4,0},{8,4},{12,8},{16,12},{20,16},{24,20},{28,24},{0,28},{5,1},{9... | collective-permute-start | bytes 3145736 | tf_op jit(solution)/shard_map/ppermute | solution.py:510
  111.4 24.1 %copy-start = (bf16[1024,512]{1,0:T(8,128)(2,1)S(1)}, bf16[1024,512]{1,0:T(8,128)(2,1)}, u32[]{:S(2)}) copy-start(bf16[1024,512]{1,0:T(8,128)(2,1)} %get-tuple-element.13) | copy-start | bytes 3145732

commit v3 on v2

--- a/solution.py
+++ b/solution.py
@@ -12,7 +12,6 @@
 MESH = pl.DeviceIdType.MESH
 TILE = 256
 PARTS = 4
-EARLY = 2
 A, B, A_FAR, B_FAR = range(4)
 
 
@@ -73,7 +72,7 @@
 def stage_kernel(num_stages, cap, ids_in, gates_in, x_hbm, dy_hbm, win_hbm, wup_hbm, wout_hbm,
                  dx_hbm, y_hbm, yx_hbm, wide_hbm, tall_hbm,
                  ids, gates, xs, dys, win, wup, wout, pos, gate_rows, pos_cols, rows, ret, rin, cin,
-                 wide_buf, tall_buf, q_early, u_early,
+                 wide_buf, tall_buf,
                  meta_send, meta_recv, hop_send, hop_recv, fwd_send, fwd_recv, dy_sem, dy_send, dy_recv,
                  ret_send, ret_recv, crs_send, crs_recv, w_sem, out_sem, res_sem, pace):
     stage, me = lax.axis_index('stage'), lax.axis_index('expert')
@@ -194,24 +193,10 @@
             meta(0, k, block).wait_recv()
     for mb in range(2):
         routing(mb, num_loc, ids, gates, pos, gate_rows, pos_cols)
-    dy_own.wait()
-    dy_near_in.wait_recv()
-    for copy in weights:
-        copy.wait()
 
     def cotangent(st):
         sel, gate = pick(pos, gate_rows, 0, st, cap)
         return sel, gate * dot(sel, dys[st // num_loc])
-
-    def early_step(st, carry):
-        q = cotangent(st)[1].astype(BF16)
-        q_early[st] = q
-        for t in range(tiles):
-            cols = slice(t * TILE, (t + 1) * TILE)
-            u_early[st, :, cols] = dot(q, wout[lax.rem(st, num_loc), cols, :], 1, 1)
-        return carry
-
-    lax.fori_loop(0, EARLY, early_step, 0)
 
     @pl.when(core == 0)
     def _():
@@ -229,6 +214,11 @@
             hop(0, k).start()
         near_arrived(0)
 
+    dy_own.wait()
+    dy_near_in.wait_recv()
+    for copy in weights:
+        copy.wait()
+
     steps = 4 * num_loc
     half, most = PARTS // 2, PARTS - 1
 
@@ -243,7 +233,7 @@
             cross(mb, k).wait_recv()
             far(mb, k).start()
 
-    def backward_step(early, st, carry):
+    def backward_step(st, carry):
         block, e = st // num_loc, lax.rem(st, num_loc)
         slot = lax.rem(st, 2)
 
@@ -308,11 +298,7 @@
             for copy in outs(st - 2):
                 copy.wait()
 
-        if early:
-            sel = pick(pos, gate_rows, 0, st, cap)[0]
-            gdy = q_early[st].astype(F32)
-        else:
-            sel, gdy = cotangent(st)
+        sel, gdy = cotangent(st)
         x = dot(sel, xs[0, block])
         tall_buf[slot, 0] = x.T.astype(BF16)
         tall_buf[slot, 1] = gdy.T.astype(BF16)
@@ -321,7 +307,7 @@
             cols = slice(t * TILE, (t + 1) * TILE)
             a = dot(x, win[e, :, cols])
             b = dot(x, wup[e, :, cols])
-            u = u_early[st, :, cols] if early else dot(q, wout[e, cols, :], 1, 1)
+            u = dot(q, wout[e, cols, :], 1, 1)
             sig = jax.nn.sigmoid(a)
             act = a * sig
             wide_buf[slot, t, 0] = (u * b * sig * (1.0 + a * (1.0 - sig))).astype(BF16)
@@ -340,8 +326,7 @@
 
         return carry
 
-    lax.fori_loop(0, EARLY, functools.partial(backward_step, True), 0)
-    lax.fori_loop(EARLY, steps, functools.partial(backward_step, False), 0)
+    lax.fori_loop(0, steps, backward_step, 0)
     for st in (steps - 2, steps - 1):
         for copy in outs(st):
             copy.wait()
@@ -456,7 +441,6 @@
             vmem((num_loc, cap, model), BF16), vmem((2, 4, tokens, model), BF16),
             vmem((2, 2, tokens, model), BF16), vmem((tokens, model), BF16),
             vmem((2, width // TILE, 3, cap, TILE), BF16), vmem((2, 2, model, cap), BF16),
-            vmem((EARLY, cap, model), BF16), vmem((EARLY, cap, width), F32),
             dma((2, 4)), dma((2, 4)), dma((2, PARTS)), dma((2, PARTS)), dma((2, 3, PARTS)), dma((2, 3, PARTS)),
             dma, dma((3,)), dma((3,)), dma((2, 2)), dma((2, 2)), dma, dma, dma((3,)), dma((2, 2)), dma((3,)),
             pltpu.SemaphoreType.REGULAR,

time: 138 us -> 139 us (level)
  no operation moved by 1% of the time
where the time goes in v3:
time: 139 us
  Pallas kernels  133 us (96%)
  starting transfers between devices  2.81 us (2%)
    pallas_call x1, Pallas kernels, stage_call(): pl.pallas_call(functools.partial(stage_kernel, num_stages, cap), out_shap...  109 us
    pallas_call x1, Pallas kernels, weight_call(): pl.pallas_call(weight_kernel, grid=(tiles,), in_specs=[pl.BlockSpec(tall....  24.1 us
  transfers between devices with their start and end apart: 2, of which 0 were waited for; matrix products, arithmetic and copies ran while one was open for 0% of the time, Pallas kernels for 17%

profile of v3, /device:TPU:1, one launch (start us, length us, event | category | flops | bytes accessed | tf_op | source)
XLA Modules:
  0.0 139.1 jit_solution(5366363344774077324)
XLA Ops:
  0.6 109.3 %stage_layer.1 = (bf16[1024,512]{1,0:T(8,128)(2,1)}, bf16[1024,512]{1,0:T(8,128)(2,1)}, bf16[1024,512]{1,0:T(8,128)(2,1)}, bf16[2,7,3,1536,256]{4,3,2,1,0:T(8,128)(2,1)}, bf16[2,2,512,1536]{3,2,1,0:T(8,128)(2,1)}) custom-call(s32[2,2,1024]{2,1,0:T(2,128)} %bitcast.13, f32[2,2,1024]{2,1,0:T(2,128)} %bitcast.14, bf16[2,1,1024,512]{3,2,1,0:T(8,128)(2,1)} %x_hbm.1, ...), custom_call_target="tpu_custom_call" | custom-call | flops 45097156608 | bytes 73400320 | tf_op jit(solution)/shard_map/stage_layer/pallas_call | solution.py:429
  110.0 2.1 %collective-permute-start = (bf16[1024,512]{1,0:T(8,128)(2,1)}, bf16[1024,512]{1,0:T(8,128)(2,1)S(1)}, u32[]{:S(2)}, u32[]{:S(2)}) collective-permute-start(bf16[1024,512]{1,0:T(8,128)(2,1)} %get-tuple-element.14), channel_id=1, source_target_pairs={{0,2},{1,3},{2,0},{3,1},{4,6},{5,7},{6,4},{7,5},{8,10},{9,11},{10,... | collective-permute-start | bytes 3145736 | tf_op jit(solution)/shard_map/ppermute | solution.py:495
  112.0 0.8 collective-permute-start.1
  112.8 0.0 copy-start
  112.8 24.1 %weight_grads.1 = (bf16[2,512,1792]{2,1,0:T(8,128)(2,1)}, bf16[2,512,1792]{2,1,0:T(8,128)(2,1)}, bf16[2,1792,512]{2,1,0:T(8,128)(2,1)}) custom-call(bf16[2,2,512,1536]{3,2,1,0:T(8,128)(2,1)} %get-tuple-element.16.tall, bf16[2,7,3,1536,256]{4,3,2,1,0:T(8,128)(2,1)} %get-tuple-element.17.wide), custom_call_target="tpu_custom_call" | custom-call | flops 16911433728 | bytes 52428800 | tf_op jit(solution)/shard_map/weight_grads/pallas_call | solution.py:465
  136.9 0.0 collective-permute-done.1
  136.9 0.0 collective-permute-done
  136.9 0.0 copy-done
  136.9 1.3 fusion
  138.1 1.0 copy.13
Async XLA Ops:
  110.0 26.9 %collective-permute-start = (bf16[1024,512]{1,0:T(8,128)(2,1)}, bf16[1024,512]{1,0:T(8,128)(2,1)S(1)}, u32[]{:S(2)}, u32[]{:S(2)}) collective-permute-start(bf16[1024,512]{1,0:T(8,128)(2,1)} %get-tuple-element.14), channel_id=1, source_target_pairs={{0,2},{1,3},{2,0},{3,1},{4,6},{5,7},{6,4},{7,5},{8,10},{9,11},{10,... | collective-permute-start | bytes 3145736 | tf_op jit(solution)/shard_map/ppermute | solution.py:495
  112.0 24.8 %collective-permute-start.1 = (bf16[1024,512]{1,0:T(8,128)(2,1)}, bf16[1024,512]{1,0:T(8,128)(2,1)S(1)}, u32[]{:S(2)}, u32[]{:S(2)}) collective-permute-start(bf16[1024,512]{1,0:T(8,128)(2,1)} %get-tuple-element.15), channel_id=1, source_target_pairs={{4,0},{8,4},{12,8},{16,12},{20,16},{24,20},{28,24},{0,28},{5,1},{9... | collective-permute-start | bytes 3145736 | tf_op jit(solution)/shard_map/ppermute | solution.py:494
  112.8 24.1 %copy-start = (bf16[1024,512]{1,0:T(8,128)(2,1)S(1)}, bf16[1024,512]{1,0:T(8,128)(2,1)}, u32[]{:S(2)}) copy-start(bf16[1024,512]{1,0:T(8,128)(2,1)} %get-tuple-element.13) | copy-start | bytes 3145732

commit v4 on v1

--- a/solution.py
+++ b/solution.py
@@ -346,9 +346,8 @@
 
     lax.fori_loop(0, EARLY, functools.partial(backward_step, True), 0)
     lax.fori_loop(EARLY, steps, functools.partial(backward_step, False), 0)
-    for st in (steps - 2, steps - 1):
-        for copy in outs(st):
-            copy.wait()
+    for copy in outs(steps - 2):
+        copy.wait()
 
     def forward_step(st, carry):
         block, e = st // num_loc, lax.rem(st, num_loc)
@@ -417,6 +416,8 @@
     ret[0, core] = add_bf16(ret.at[0, core], rin.at[0, 0], cin)
     dx_save.start()
 
+    for copy in outs(steps - 1):
+        copy.wait()
     for flip in range(4):
         for k in range(2):
             meta(flip, k).wait_send()

time: 138 us -> 138 us (level)
  no operation moved by 1% of the time
where the time goes in v4:
time: 138 us; the launch traced here: 137 us
  Pallas kernels  132 us (96%)
  starting transfers between devices  2.82 us (2%)
    pallas_call x1, Pallas kernels, stage_call(): pl.pallas_call(functools.partial(stage_kernel, num_stages, cap), out_shap...  108 us
    pallas_call x1, Pallas kernels, weight_call(): pl.pallas_call(weight_kernel, grid=(tiles,), in_specs=[pl.BlockSpec(tall....  24.1 us
  transfers between devices with their start and end apart: 2, of which 0 were waited for; matrix products, arithmetic and copies ran while one was open for 0% of the time, Pallas kernels for 18%

profile of v4, /device:TPU:1, one launch (start us, length us, event | category | flops | bytes accessed | tf_op | source)
XLA Modules:
  0.0 137.4 jit_solution(7395845731860209116)
XLA Ops:
  0.6 107.6 %stage_layer.1 = (bf16[1024,512]{1,0:T(8,128)(2,1)}, bf16[1024,512]{1,0:T(8,128)(2,1)}, bf16[1024,512]{1,0:T(8,128)(2,1)}, bf16[2,7,3,1536,256]{4,3,2,1,0:T(8,128)(2,1)}, bf16[2,2,512,1536]{3,2,1,0:T(8,128)(2,1)}) custom-call(s32[2,2,1024]{2,1,0:T(2,128)} %bitcast.13, f32[2,2,1024]{2,1,0:T(2,128)} %bitcast.14, bf16[2,1,1024,512]{3,2,1,0:T(8,128)(2,1)} %x_hbm.1, ...), custom_call_target="tpu_custom_call" | custom-call | flops 45097156608 | bytes 73400320 | tf_op jit(solution)/shard_map/stage_layer/pallas_call | solution.py:449
  108.3 2.1 %collective-permute-start = (bf16[1024,512]{1,0:T(8,128)(2,1)}, bf16[1024,512]{1,0:T(8,128)(2,1)S(1)}, u32[]{:S(2)}, u32[]{:S(2)}) collective-permute-start(bf16[1024,512]{1,0:T(8,128)(2,1)} %get-tuple-element.14), channel_id=1, source_target_pairs={{0,2},{1,3},{2,0},{3,1},{4,6},{5,7},{6,4},{7,5},{8,10},{9,11},{10,... | collective-permute-start | bytes 3145736 | tf_op jit(solution)/shard_map/ppermute | solution.py:516
  110.3 0.8 collective-permute-start.1
  111.1 0.0 copy-start
  111.1 24.1 %weight_grads.1 = (bf16[2,512,1792]{2,1,0:T(8,128)(2,1)}, bf16[2,512,1792]{2,1,0:T(8,128)(2,1)}, bf16[2,1792,512]{2,1,0:T(8,128)(2,1)}) custom-call(bf16[2,2,512,1536]{3,2,1,0:T(8,128)(2,1)} %get-tuple-element.16.tall, bf16[2,7,3,1536,256]{4,3,2,1,0:T(8,128)(2,1)} %get-tuple-element.17.wide), custom_call_target="tpu_custom_call" | custom-call | flops 16911433728 | bytes 52428800 | tf_op jit(solution)/shard_map/weight_grads/pallas_call | solution.py:486
  135.2 0.0 collective-permute-done.1
  135.2 0.0 collective-permute-done
  135.2 0.0 copy-done
  135.2 1.3 fusion
  136.4 1.0 copy.13
Async XLA Ops:
  108.3 26.9 %collective-permute-start = (bf16[1024,512]{1,0:T(8,128)(2,1)}, bf16[1024,512]{1,0:T(8,128)(2,1)S(1)}, u32[]{:S(2)}, u32[]{:S(2)}) collective-permute-start(bf16[1024,512]{1,0:T(8,128)(2,1)} %get-tuple-element.14), channel_id=1, source_target_pairs={{0,2},{1,3},{2,0},{3,1},{4,6},{5,7},{6,4},{7,5},{8,10},{9,11},{10,... | collective-permute-start | bytes 3145736 | tf_op jit(solution)/shard_map/ppermute | solution.py:516
  110.3 24.8 %collective-permute-start.1 = (bf16[1024,512]{1,0:T(8,128)(2,1)}, bf16[1024,512]{1,0:T(8,128)(2,1)S(1)}, u32[]{:S(2)}, u32[]{:S(2)}) collective-permute-start(bf16[1024,512]{1,0:T(8,128)(2,1)} %get-tuple-element.15), channel_id=1, source_target_pairs={{4,0},{8,4},{12,8},{16,12},{20,16},{24,20},{28,24},{0,28},{5,1},{9... | collective-permute-start | bytes 3145736 | tf_op jit(solution)/shard_map/ppermute | solution.py:515
  111.1 24.1 %copy-start = (bf16[1024,512]{1,0:T(8,128)(2,1)S(1)}, bf16[1024,512]{1,0:T(8,128)(2,1)}, u32[]{:S(2)}) copy-start(bf16[1024,512]{1,0:T(8,128)(2,1)} %get-tuple-element.13) | copy-start | bytes 3145732

commit v5 on v4

--- a/solution.py
+++ b/solution.py
@@ -56,9 +56,9 @@
     part = out.shape[2] // PARTS
     for m in range(PARTS):
         span = slice(m * part, (m + 1) * part)
-        cols = pltpu.roll(pos_cols[mb, span, :], lax.rem(128 - num_loc * block, 128), 1)
         slot = lax.broadcasted_iota(jnp.int32, (part, cap), 1)
-        sel = [jnp.where(cols[:, e:e + 1] == slot, 1.0, 0.0).astype(BF16) for e in range(num_loc)]
+        cols = [pos_cols[mb, span, num_loc * block + e:num_loc * block + e + 1] for e in range(num_loc)]
+        sel = [jnp.where(col == slot, 1.0, 0.0).astype(BF16) for col in cols]
         total = dot(jnp.concatenate(sel, axis=1), rows[...].reshape(num_loc * cap, rows.shape[2]))
         out[mb, block, span, :] = total.astype(BF16)
 
@@ -139,10 +139,15 @@
         src = ret.at[mb, 2 * k + other if block is None else block]
         return remote(src, rin.at[mb, k], ret_send.at[mb, k], ret_recv.at[mb, k], partner)
 
-    def send_back(mb, block):
-        @pl.when(lax.rem(block, 2) != core)
-        def _():
-            back(mb, block // 2, block).start()
+    def finish_block(mb, st, blocks):
+        for block in blocks:
+            @pl.when(st == (block + 1) * num_loc - 1)
+            def _(block=block):
+                to_tokens(pos_cols, mb, block, rows, ret)
+
+                @pl.when(core != block % 2)
+                def _():
+                    back(mb, block // 2, block).start()
 
     dx_cross = remote(ret.at[0, 2 + core], cin, crs_send, crs_recv, across)
 
@@ -337,10 +342,7 @@
         for copy in outs(st):
             copy.start()
 
-        @pl.when(e == num_loc - 1)
-        def _():
-            to_tokens(pos_cols, 0, block, rows, ret)
-            send_back(0, block)
+        finish_block(0, st, range(EARLY // num_loc) if early else range(EARLY // num_loc, 4))
 
         return carry
 
@@ -400,10 +402,7 @@
         hid = jnp.concatenate([wide_buf[0, t, 0] for t in range(tiles)], axis=1)
         rows[e] = (gate * dot(hid, wout[e])).astype(BF16)
 
-        @pl.when(e == num_loc - 1)
-        def _():
-            to_tokens(pos_cols, 1, block, rows, ret)
-            send_back(1, block)
+        finish_block(1, st, range(4))
 
         return carry
 

time: 138 us -> 137 us (level)
  no operation moved by 1% of the time
where the time goes in v5:
time: 137 us
  Pallas kernels  131 us (96%)
  starting transfers between devices  2.81 us (2%)
    pallas_call x1, Pallas kernels, stage_call(): pl.pallas_call(functools.partial(stage_kernel, num_stages, cap), out_shap...  107 us
    pallas_call x1, Pallas kernels, weight_call(): pl.pallas_call(weight_kernel, grid=(tiles,), in_specs=[pl.BlockSpec(tall....  24.1 us
  transfers between devices with their start and end apart: 2, of which 0 were waited for; matrix products, arithmetic and copies ran while one was open for 0% of the time, Pallas kernels for 18%

profile of v5, /device:TPU:1, one launch (start us, length us, event | category | flops | bytes accessed | tf_op | source)
XLA Modules:
  0.0 136.9 jit_solution(18164062546198755513)
XLA Ops:
  0.6 107.1 %stage_layer.1 = (bf16[1024,512]{1,0:T(8,128)(2,1)}, bf16[1024,512]{1,0:T(8,128)(2,1)}, bf16[1024,512]{1,0:T(8,128)(2,1)}, bf16[2,7,3,1536,256]{4,3,2,1,0:T(8,128)(2,1)}, bf16[2,2,512,1536]{3,2,1,0:T(8,128)(2,1)}) custom-call(s32[2,2,1024]{2,1,0:T(2,128)} %bitcast.13, f32[2,2,1024]{2,1,0:T(2,128)} %bitcast.14, bf16[2,1,1024,512]{3,2,1,0:T(8,128)(2,1)} %x_hbm.1, ...), custom_call_target="tpu_custom_call" | custom-call | flops 45097156608 | bytes 73400320 | tf_op jit(solution)/shard_map/stage_layer/pallas_call | solution.py:448
  107.8 2.1 %collective-permute-start = (bf16[1024,512]{1,0:T(8,128)(2,1)}, bf16[1024,512]{1,0:T(8,128)(2,1)S(1)}, u32[]{:S(2)}, u32[]{:S(2)}) collective-permute-start(bf16[1024,512]{1,0:T(8,128)(2,1)} %get-tuple-element.14), channel_id=1, source_target_pairs={{0,2},{1,3},{2,0},{3,1},{4,6},{5,7},{6,4},{7,5},{8,10},{9,11},{10,... | collective-permute-start | bytes 3145736 | tf_op jit(solution)/shard_map/ppermute | solution.py:515
  109.8 0.8 collective-permute-start.1
  110.6 0.0 copy-start
  110.6 24.1 %weight_grads.1 = (bf16[2,512,1792]{2,1,0:T(8,128)(2,1)}, bf16[2,512,1792]{2,1,0:T(8,128)(2,1)}, bf16[2,1792,512]{2,1,0:T(8,128)(2,1)}) custom-call(bf16[2,2,512,1536]{3,2,1,0:T(8,128)(2,1)} %get-tuple-element.16.tall, bf16[2,7,3,1536,256]{4,3,2,1,0:T(8,128)(2,1)} %get-tuple-element.17.wide), custom_call_target="tpu_custom_call" | custom-call | flops 16911433728 | bytes 52428800 | tf_op jit(solution)/shard_map/weight_grads/pallas_call | solution.py:485
  134.7 0.0 collective-permute-done.1
  134.7 0.0 collective-permute-done
  134.7 0.0 copy-done
  134.7 1.3 fusion
  135.9 1.0 copy.13
Async XLA Ops:
  107.8 26.9 %collective-permute-start = (bf16[1024,512]{1,0:T(8,128)(2,1)}, bf16[1024,512]{1,0:T(8,128)(2,1)S(1)}, u32[]{:S(2)}, u32[]{:S(2)}) collective-permute-start(bf16[1024,512]{1,0:T(8,128)(2,1)} %get-tuple-element.14), channel_id=1, source_target_pairs={{0,2},{1,3},{2,0},{3,1},{4,6},{5,7},{6,4},{7,5},{8,10},{9,11},{10,... | collective-permute-start | bytes 3145736 | tf_op jit(solution)/shard_map/ppermute | solution.py:515
  109.8 24.8 %collective-permute-start.1 = (bf16[1024,512]{1,0:T(8,128)(2,1)}, bf16[1024,512]{1,0:T(8,128)(2,1)S(1)}, u32[]{:S(2)}, u32[]{:S(2)}) collective-permute-start(bf16[1024,512]{1,0:T(8,128)(2,1)} %get-tuple-element.15), channel_id=1, source_target_pairs={{4,0},{8,4},{12,8},{16,12},{20,16},{24,20},{28,24},{0,28},{5,1},{9... | collective-permute-start | bytes 3145736 | tf_op jit(solution)/shard_map/ppermute | solution.py:514
  110.6 24.1 %copy-start = (bf16[1024,512]{1,0:T(8,128)(2,1)S(1)}, bf16[1024,512]{1,0:T(8,128)(2,1)}, u32[]{:S(2)}) copy-start(bf16[1024,512]{1,0:T(8,128)(2,1)} %get-tuple-element.13) | copy-start | bytes 3145732
